TPU v7x, 32 devices: a whole 2x2x4 slice. The times are simulated.
32 devices in a mesh: unit: 4 (over y, core), zero: 4 (over z), cols: 2 (over x).
Axes of the slice: x: 2, y: 2, z: 4, core: 2. Of those that a mesh axis runs over, the one named last changes fastest.
Arguments:
- weight_gate: bfloat16 [20480, 13824], P(('unit', 'zero'), 'cols'), parts along dimension 0, may hold values from -0.125 to 0.125
- low_gate: bfloat16 [20480, 32], P(('unit', 'zero')), parts along dimension 0, may hold values from -0.078125 to 0.078125
- high_gate: bfloat16 [128, 13824], P('unit', 'cols'), parts along dimension 0, may hold values from -1 to 1
- weight_up: bfloat16 [20480, 13824], P(('unit', 'zero'), 'cols'), parts along dimension 0, may hold values from -0.125 to 0.125
- low_up: bfloat16 [20480, 32], P(('unit', 'zero')), parts along dimension 0, may hold values from -0.078125 to 0.078125
- high_up: bfloat16 [128, 13824], P('unit', 'cols'), parts along dimension 0, may hold values from -1 to 1
- norm_train: float32 [20480], P(('unit', 'zero', 'cols')), parts along dimension 0, may hold values from 0.25 to 1.75
- norm_step: float32 [20480], P(('unit', 'zero', 'cols')), parts along dimension 0, may hold values from -0.3 to 0.3
Outputs:
- final_gate: bfloat16 [20480, 13824], P('unit', ('cols', 'zero')), parts along dimension 0
- final_up: bfloat16 [20480, 13824], P('unit', ('cols', 'zero')), parts along dimension 0
- scale_gate: float32 [55296], P(('unit', 'cols', 'zero')), parts along dimension 0
- scale_up: float32 [55296], P(('unit', 'cols', 'zero')), parts along dimension 0
- serve_norm: bfloat16 [20480], P('unit'), parts along dimension 0
There are 4 independent parts, one for each index of `unit`. A program takes and returns all parts, laid end to end along the dimension named above; each array names one. Nothing has to cross between parts.
All inputs are finite; a program needn't handle non-finite values. Where the computation divides by a largest or mean magnitude, that divisor is 1e-20 or more.
Results may differ from a plain program's by a relative error of at most 0.001.
Values may be sent and summed in bfloat16 or wider, within the bound.
A program may use at most 192 MiB of HBM per device.

v0:
```python
import jax
import jax.numpy as jnp
from jax import lax
from jax.sharding import PartitionSpec as P

D_MODEL = 5120
mix_rate = 0.5


def local(weight_gate, low_gate, high_gate, weight_up, low_up, high_up, norm_train, norm_step):
    result_gate = weight_gate.astype(jnp.float32) + mix_rate * jnp.dot(
        low_gate, high_gate, preferred_element_type=jnp.float32
    )
    result_up = weight_up.astype(jnp.float32) + mix_rate * jnp.dot(
        low_up, high_up, preferred_element_type=jnp.float32
    )
    total_gate, total_up = lax.psum(
        (jnp.sum(jnp.abs(result_gate), axis=0), jnp.sum(jnp.abs(result_up), axis=0)), "zero"
    )
    scale_gate = total_gate / D_MODEL
    scale_up = total_up / D_MODEL
    narrow_gate, narrow_up = (
        (result_gate / scale_gate).astype(jnp.bfloat16),
        (result_up / scale_up).astype(jnp.bfloat16),
    )
    final_gate, final_up = (
        lax.all_to_all(narrow_gate, "zero", split_axis=1, concat_axis=0, tiled=True),
        lax.all_to_all(narrow_up, "zero", split_axis=1, concat_axis=0, tiled=True),
    )
    place = lax.axis_index("zero")
    scale_gate = lax.dynamic_slice_in_dim(
        scale_gate, place * final_gate.shape[1], final_gate.shape[1]
    )
    scale_up = lax.dynamic_slice_in_dim(scale_up, place * final_up.shape[1], final_up.shape[1])
    serve_norm = lax.all_gather(
        (norm_train + norm_step).astype(jnp.bfloat16), ("zero", "cols"), axis=0, tiled=True
    )
    return (final_gate, final_up, scale_gate, scale_up, serve_norm)


def solution(mesh):
    in_specs = (
        P(("unit", "zero"), "cols"),
        P(("unit", "zero"), None),
        P("unit", "cols"),
        P(("unit", "zero"), "cols"),
        P(("unit", "zero"), None),
        P("unit", "cols"),
        P(("unit", "zero", "cols")),
        P(("unit", "zero", "cols")),
    )
    out_specs = (
        P("unit", ("cols", "zero")),
        P("unit", ("cols", "zero")),
        P(("unit", "cols", "zero")),
        P(("unit", "cols", "zero")),
        P("unit"),
    )
    return jax.shard_map(local, mesh=mesh, in_specs=in_specs, out_specs=out_specs, check_vma=False)
```

profile of v0, /device:TPU:0, one launch (start us, length us, event | category | flops | bytes accessed | tf_op | source)
XLA Modules:
  0.0 996.0 jit_solution(447909113472326274)
XLA Ops:
  0.6 0.0 copy-start
  0.6 0.0 copy-start.3
  0.7 0.0 copy-start.2
  0.7 1.0 copy-done
  1.7 17.9 %abs_reduce_fusion.1 = (f32[6912]{0:T(1024)S(1)}, f32[1280,6912]{1,0:T(8,128)}) fusion(bf16[1280,32]{0,1:T(8,128)(2,1)} %param.9, bf16[32,6912]{1,0:T(8,128)(2,1)S(1)} %copy-done, bf16[1280,6912]{1,0:T(8,128)(2,1)} %param.8), kind=kOutput, calls=%fused_computation.4 | convolution fusion | flops 610460928 | bytes 53636096 | tf_op jit(solution)/shard_map/dot_general | solution.py:11
  19.6 18.0 %abs_reduce_fusion = (f32[6912]{0:T(1024)S(1)}, f32[1280,6912]{1,0:T(8,128)}) fusion(bf16[1280,32]{0,1:T(8,128)(2,1)S(1)} %copy-done.3, bf16[32,6912]{1,0:T(8,128)(2,1)S(1)} %copy-done.2, bf16[1280,6912]{1,0:T(8,128)(2,1)} %param.11), kind=kOutput, calls=%fused_computation.1 | convolution fusion | flops 610460928 | bytes 53636096 | tf_op jit(solution)/shard_map/dot_general | solution.py:14
  37.6 21.7 %all-reduce = (f32[6912]{0:T(1024)S(1)}, f32[6912]{0:T(1024)S(1)}) all-reduce(f32[6912]{0:T(1024)S(1)} %get-tuple-element.17, f32[6912]{0:T(1024)S(1)} %get-tuple-element.19), channel_id=1, replica_groups=mesh['unit'=4,'zero'=4,'cols'=2] {'zero'}, use_global_device_ids=true, to_apply=%region_1.0 | all-reduce | flops 13824 | bytes 110592 | tf_op jit(solution)/shard_map/psum | solution.py:17
  59.3 19.8 %divide_convert_fusion.1 = bf16[1280,6912]{1,0:T(8,128)(2,1)} fusion(f32[1280,6912]{1,0:T(8,128)} %get-tuple-element.18, f32[6912]{0:T(1024)S(1)} %get-tuple-element.22), kind=kLoop, calls=%fused_computation.3 | loop fusion | flops 17694720 | bytes 53111808 | tf_op jit(solution)/shard_map/convert_element_type | solution.py:23
  79.1 24.6 %copy.23 = bf16[1280,6912]{0,1:T(8,128)(2,1)} copy(bf16[1280,6912]{1,0:T(8,128)(2,1)} %divide_convert_fusion.1) | data formatting | bytes 35389440 | tf_op jit(solution)/shard_map/convert_element_type | solution.py:23
  103.7 7.2 all-to-all-start
  110.9 19.8 %divide_convert_fusion = bf16[1280,6912]{1,0:T(8,128)(2,1)} fusion(f32[1280,6912]{1,0:T(8,128)} %get-tuple-element.20, f32[6912]{0:T(1024)S(1)} %get-tuple-element.21), kind=kLoop, calls=%fused_computation | loop fusion | flops 17694720 | bytes 53111808 | tf_op jit(solution)/shard_map/convert_element_type | solution.py:24
  130.7 23.0 %copy.25 = bf16[1280,6912]{0,1:T(8,128)(2,1)} copy(bf16[1280,6912]{1,0:T(8,128)(2,1)} %divide_convert_fusion) | data formatting | bytes 35389440 | tf_op jit(solution)/shard_map/convert_element_type | solution.py:24
  153.7 335.9 %all-to-all-done = bf16[1280,4,1728]{0,2,1:T(8,128)(2,1)} async-done(((bf16[1280,4,1728]{0,2,1:T(8,128)(2,1)}), bf16[1280,4,1728]{0,2,1:T(8,128)(2,1)}, u32[]{:S(2)}, u32[]{:S(2)}) %all-to-all-start) | async-done | bytes 17694752 | tf_op jit(solution)/shard_map/all_to_all | solution.py:27
  489.6 7.2 all-to-all-start.1
  496.8 0.7 dynamic_slice.6
  497.5 0.7 dynamic_slice.7
  498.2 400.5 %all-gather = bf16[8,1,640]{2,1,0:T(2,128)(2,1)S(1)} all-gather(bf16[1,1,640]{2,1,0:T(2,128)(2,1)S(1)} %reshape.18), channel_id=1, replica_groups=mesh['unit'=4,'zero'=4,'cols'=2] {'zero','cols'}, dimensions={0}, use_global_device_ids=true | all-gather | bytes 11520 | tf_op jit(solution)/shard_map/all_gather | solution.py:35
  898.8 0.1 reduce
  898.8 0.6 reshape.19
  899.4 23.3 %copy.24 = bf16[4,1280,1728]{2,1,0:T(8,128)(2,1)} copy(bf16[4,1280,1728]{1,2,0:T(8,128)(2,1)} %bitcast.1) | data formatting | bytes 35389440 | tf_op jit(solution)/shard_map/all_to_all | solution.py:27
  922.8 24.9 %copy.27 = bf16[5120,1728]{0,1:T(8,128)(2,1)} copy(bf16[5120,1728]{1,0:T(8,128)(2,1)} %bitcast.10) | data formatting | bytes 35389440
  947.7 0.0 all-to-all-done.1
  947.7 23.4 %copy.26 = bf16[4,1280,1728]{2,1,0:T(8,128)(2,1)} copy(bf16[4,1280,1728]{1,2,0:T(8,128)(2,1)} %bitcast.4) | data formatting | bytes 35389440 | tf_op jit(solution)/shard_map/all_to_all | solution.py:28
  971.1 24.9 %copy.28 = bf16[5120,1728]{0,1:T(8,128)(2,1)} copy(bf16[5120,1728]{1,0:T(8,128)(2,1)} %bitcast.11) | data formatting | bytes 35389440
  (11 shorter events, 0.0 us)
Async XLA Ops:
  0.6 1.0 copy-start
  0.6 18.9 %copy-start.3 = (bf16[1280,32]{0,1:T(8,128)(2,1)S(1)}, bf16[1280,32]{0,1:T(8,128)(2,1)}, u32[]{:S(2)}) copy-start(bf16[1280,32]{0,1:T(8,128)(2,1)} %param.12) | copy-start | bytes 245764
  0.7 18.9 %copy-start.2 = (bf16[32,6912]{1,0:T(8,128)(2,1)S(1)}, bf16[32,6912]{1,0:T(8,128)(2,1)}, u32[]{:S(2)}) copy-start(bf16[32,6912]{1,0:T(8,128)(2,1)} %param.13) | copy-start | bytes 1327108
  103.7 385.9 %all-to-all-start = ((bf16[1280,4,1728]{0,2,1:T(8,128)(2,1)}), bf16[1280,4,1728]{0,2,1:T(8,128)(2,1)}, u32[]{:S(2)}, u32[]{:S(2)}) async-start(bf16[1280,4,1728]{0,2,1:T(8,128)(2,1)} %bitcast.13), calls=%async_computation | async-start | bytes 35389440 | tf_op jit(solution)/shard_map/all_to_all | solution.py:27
  130.7 367.5 %copy-start.4 = (f32[640]{0:T(1024)S(1)}, f32[640]{0:T(1024)}, u32[]{:S(2)}) copy-start(f32[640]{0:T(1024)} %param.14) | copy-start | bytes 7684
  130.7 367.5 %copy-start.5 = (f32[640]{0:T(1024)S(1)}, f32[640]{0:T(1024)}, u32[]{:S(2)}) copy-start(f32[640]{0:T(1024)} %param.15) | copy-start | bytes 7684
  489.6 458.1 %all-to-all-start.1 = ((bf16[1280,4,1728]{0,2,1:T(8,128)(2,1)}), bf16[1280,4,1728]{0,2,1:T(8,128)(2,1)}, u32[]{:S(2)}, u32[]{:S(2)}) async-start(bf16[1280,4,1728]{0,2,1:T(8,128)(2,1)} %bitcast.12), calls=%async_computation.1 | async-start | bytes 35389440 | tf_op jit(solution)/shard_map/all_to_all | solution.py:28
  947.7 48.3 %copy-start.1 = (bf16[32,6912]{1,0:T(8,128)(2,1)S(1)}, bf16[32,6912]{1,0:T(8,128)(2,1)}, u32[]{:S(2)}) copy-start(bf16[32,6912]{1,0:T(8,128)(2,1)} %param.10) | copy-start | bytes 1327108
where the time goes:
time: 1000 us; the launch traced here: 996 us
  blocking collectives  422 us (42%)
  waiting for transfers between devices  336 us (34%)
  local copies, waits for them, and re-layouts  147 us (15%)
  other arithmetic  39.7 us (4%)
  matrix products  35.9 us (4%)
  starting transfers between devices  14.4 us (1%)
    all_gather x1, blocking collectives, local(): lax.all_gather((norm_train + norm_step).astype(jnp.bfloat16), ('zero', 'c...  401 us
    all_to_all x1, waiting for transfers between devices, local(): lax.all_to_all(narrow_gate, 'zero', split_axis=1, concat_axis=0, tiled=True)  336 us
    unnamed x16, local copies, waits for them, and re-layouts  51.5 us
    convert_element_type x1, local copies, waits for them, and re-layouts, local(): (result_gate / scale_gate).astype(jnp.bfloat16)  24.6 us
    all_to_all x1, local copies, waits for them, and re-layouts, local(): lax.all_to_all(narrow_up, 'zero', split_axis=1, concat_axis=0, tiled=True)  23.4 us
    all_to_all x1, local copies, waits for them, and re-layouts, local(): lax.all_to_all(narrow_gate, 'zero', split_axis=1, concat_axis=0, tiled=True)  23.3 us
    convert_element_type x1, local copies, waits for them, and re-layouts, local(): (result_up / scale_up).astype(jnp.bfloat16)  23 us
    psum x1, blocking collectives, local(): lax.psum((jnp.sum(jnp.abs(result_gate), axis=0), jnp.sum(jnp.abs(result_u...  21.7 us
  transfers between devices with their start and end apart: 2, of which 1 were waited for; matrix products, arithmetic and copies ran while one was open for 9% of the time, Pallas kernels for 0%

commit v1 on v0

--- a/solution.py
+++ b/solution.py
@@ -32,8 +32,16 @@
         scale_gate, place * final_gate.shape[1], final_gate.shape[1]
     )
     scale_up = lax.dynamic_slice_in_dim(scale_up, place * final_up.shape[1], final_up.shape[1])
-    serve_norm = lax.all_gather(
-        (norm_train + norm_step).astype(jnp.bfloat16), ("zero", "cols"), axis=0, tiled=True
+    serve_norm = jnp.concatenate(
+        lax.all_to_all(
+            jnp.stack(
+                [(norm_train + norm_step).astype(jnp.bfloat16)] * lax.axis_size(("zero", "cols"))
+            ),
+            ("zero", "cols"),
+            0,
+            0,
+        ),
+        axis=0,
     )
     return (final_gate, final_up, scale_gate, scale_up, serve_norm)
 

time: 1000 us -> 938 us (0.938)
  blocking collectives: 422 us -> 20.1 us
  waiting for transfers between devices: 336 us -> 667 us
    all_gather x1 -> x0, blocking collectives: 401 us -> none  [local(): lax.all_gather((norm_train + norm_step).astype(jnp.bfloat16), ('zero', 'c...]
    all_to_all x1, waiting for transfers between devices: 0.01 us -> 332 us  [local(): lax.all_to_all(narrow_up, 'zero', split_axis=1, concat_axis=0, tiled=True)]
    unnamed x16 -> x12, local copies, waits for them, and re-layouts: 51.5 us -> 50.6 us
  transfers between devices with their start and end apart: 2 -> 3, of which waited for: 1 -> 2; matrix products, arithmetic and copies ran while one was open for 9% -> 19% of each run, Pallas kernels for 0% -> 0%
where the time goes in v1:
time: 938 us; the launch traced here: 934 us
  waiting for transfers between devices  667 us (71%)
  local copies, waits for them, and re-layouts  147 us (16%)
  other arithmetic  41.1 us (4%)
  matrix products  35.8 us (4%)
  starting transfers between devices  21.6 us (2%)
  blocking collectives  20.1 us (2%)
    all_to_all x1, waiting for transfers between devices, local(): lax.all_to_all(narrow_gate, 'zero', split_axis=1, concat_axis=0, tiled=True)  336 us
    all_to_all x1, waiting for transfers between devices, local(): lax.all_to_all(narrow_up, 'zero', split_axis=1, concat_axis=0, tiled=True)  332 us
    unnamed x12, local copies, waits for them, and re-layouts  50.6 us
    convert_element_type x1, local copies, waits for them, and re-layouts, local(): (result_gate / scale_gate).astype(jnp.bfloat16)  24.6 us
    all_to_all x1, local copies, waits for them, and re-layouts, local(): lax.all_to_all(narrow_up, 'zero', split_axis=1, concat_axis=0, tiled=True)  23.4 us
    all_to_all x1, local copies, waits for them, and re-layouts, local(): lax.all_to_all(narrow_gate, 'zero', split_axis=1, concat_axis=0, tiled=True)  23.3 us
    convert_element_type x1, local copies, waits for them, and re-layouts, local(): (result_up / scale_up).astype(jnp.bfloat16)  23 us
    psum x1, blocking collectives, local(): lax.psum((jnp.sum(jnp.abs(result_gate), axis=0), jnp.sum(jnp.abs(result_u...  20.1 us
  transfers between devices with their start and end apart: 3, of which 2 were waited for; matrix products, arithmetic and copies ran while one was open for 19% of the time, Pallas kernels for 0%

profile of v1, /device:TPU:0, one launch (start us, length us, event | category | flops | bytes accessed | tf_op | source)
XLA Modules:
  0.0 934.2 jit_solution(2332191974616088017)
XLA Ops:
  0.7 0.8 add_convert_fusion
  1.5 0.5 broadcast.21
  2.0 0.7 reduce.1
  2.7 0.7 reshape.31
  3.4 7.3 all-to-all-start.2
  10.7 17.9 %abs_reduce_fusion.1 = (f32[6912]{0:T(1024)S(1)}, f32[1280,6912]{1,0:T(8,128)}) fusion(bf16[1280,32]{0,1:T(8,128)(2,1)} %param.9, bf16[32,6912]{1,0:T(8,128)(2,1)S(1)} %copy-done, bf16[1280,6912]{1,0:T(8,128)(2,1)} %param.8), kind=kOutput, calls=%fused_computation.4 | convolution fusion | flops 610460928 | bytes 53636096 | tf_op jit(solution)/shard_map/dot_general | solution.py:11
  28.6 17.9 %abs_reduce_fusion = (f32[6912]{0:T(1024)S(1)}, f32[1280,6912]{1,0:T(8,128)}) fusion(bf16[1280,32]{0,1:T(8,128)(2,1)S(1)} %copy-done.3, bf16[32,6912]{1,0:T(8,128)(2,1)S(1)} %copy-done.2, bf16[1280,6912]{1,0:T(8,128)(2,1)} %param.11), kind=kOutput, calls=%fused_computation.1 | convolution fusion | flops 610460928 | bytes 53636096 | tf_op jit(solution)/shard_map/dot_general | solution.py:14
  46.5 20.1 %all-reduce = (f32[6912]{0:T(1024)S(1)}, f32[6912]{0:T(1024)S(1)}) all-reduce(f32[6912]{0:T(1024)S(1)} %get-tuple-element.17, f32[6912]{0:T(1024)S(1)} %get-tuple-element.19), channel_id=1, replica_groups=mesh['unit'=4,'zero'=4,'cols'=2] {'zero'}, use_global_device_ids=true, to_apply=%region_1.0 | all-reduce | flops 13824 | bytes 110592 | tf_op jit(solution)/shard_map/psum | solution.py:17
  66.7 19.8 %divide_convert_fusion.1 = bf16[1280,6912]{1,0:T(8,128)(2,1)} fusion(f32[1280,6912]{1,0:T(8,128)} %get-tuple-element.18, f32[6912]{0:T(1024)S(1)} %get-tuple-element.22), kind=kLoop, calls=%fused_computation.3 | loop fusion | flops 17694720 | bytes 53111808 | tf_op jit(solution)/shard_map/convert_element_type | solution.py:23
  86.4 24.6 %copy.23 = bf16[1280,6912]{0,1:T(8,128)(2,1)} copy(bf16[1280,6912]{1,0:T(8,128)(2,1)} %divide_convert_fusion.1) | data formatting | bytes 35389440 | tf_op jit(solution)/shard_map/convert_element_type | solution.py:23
  111.1 7.2 all-to-all-start
  118.2 19.8 %divide_convert_fusion = bf16[1280,6912]{1,0:T(8,128)(2,1)} fusion(f32[1280,6912]{1,0:T(8,128)} %get-tuple-element.20, f32[6912]{0:T(1024)S(1)} %get-tuple-element.21), kind=kLoop, calls=%fused_computation | loop fusion | flops 17694720 | bytes 53111808 | tf_op jit(solution)/shard_map/convert_element_type | solution.py:24
  138.0 23.0 %copy.25 = bf16[1280,6912]{0,1:T(8,128)(2,1)} copy(bf16[1280,6912]{1,0:T(8,128)(2,1)} %divide_convert_fusion) | data formatting | bytes 35389440 | tf_op jit(solution)/shard_map/convert_element_type | solution.py:24
  161.0 335.7 %all-to-all-done = bf16[1280,4,1728]{0,2,1:T(8,128)(2,1)} async-done(((bf16[1280,4,1728]{0,2,1:T(8,128)(2,1)}), bf16[1280,4,1728]{0,2,1:T(8,128)(2,1)}, u32[]{:S(2)}, u32[]{:S(2)}) %all-to-all-start) | async-done | bytes 17694752 | tf_op jit(solution)/shard_map/all_to_all | solution.py:27
  496.7 7.2 all-to-all-start.1
  503.9 0.7 dynamic_slice.6
  504.6 0.7 dynamic_slice.7
  505.3 0.1 reshape.32
  505.4 0.6 reshape.29
  506.0 23.3 %copy.24 = bf16[4,1280,1728]{2,1,0:T(8,128)(2,1)} copy(bf16[4,1280,1728]{1,2,0:T(8,128)(2,1)} %bitcast.1) | data formatting | bytes 35389440 | tf_op jit(solution)/shard_map/all_to_all | solution.py:27
  529.3 24.9 %copy.27 = bf16[5120,1728]{0,1:T(8,128)(2,1)} copy(bf16[5120,1728]{1,0:T(8,128)(2,1)} %bitcast.10) | data formatting | bytes 35389440
  554.3 331.7 %all-to-all-done.1 = bf16[1280,4,1728]{0,2,1:T(8,128)(2,1)} async-done(((bf16[1280,4,1728]{0,2,1:T(8,128)(2,1)}), bf16[1280,4,1728]{0,2,1:T(8,128)(2,1)}, u32[]{:S(2)}, u32[]{:S(2)}) %all-to-all-start.1) | async-done | bytes 17694752 | tf_op jit(solution)/shard_map/all_to_all | solution.py:28
  886.0 23.4 %copy.26 = bf16[4,1280,1728]{2,1,0:T(8,128)(2,1)} copy(bf16[4,1280,1728]{1,2,0:T(8,128)(2,1)} %bitcast.4) | data formatting | bytes 35389440 | tf_op jit(solution)/shard_map/all_to_all | solution.py:28
  909.3 24.9 %copy.28 = bf16[5120,1728]{0,1:T(8,128)(2,1)} copy(bf16[5120,1728]{1,0:T(8,128)(2,1)} %bitcast.11) | data formatting | bytes 35389440
  (12 shorter events, 0.1 us)
Async XLA Ops:
  0.6 10.0 %copy-start = (bf16[32,6912]{1,0:T(8,128)(2,1)S(1)}, bf16[32,6912]{1,0:T(8,128)(2,1)}, u32[]{:S(2)}) copy-start(bf16[32,6912]{1,0:T(8,128)(2,1)} %param.10) | copy-start | bytes 1327108
  0.6 28.0 %copy-start.3 = (bf16[1280,32]{0,1:T(8,128)(2,1)S(1)}, bf16[1280,32]{0,1:T(8,128)(2,1)}, u32[]{:S(2)}) copy-start(bf16[1280,32]{0,1:T(8,128)(2,1)} %param.12) | copy-start | bytes 245764
  0.7 28.0 %copy-start.2 = (bf16[32,6912]{1,0:T(8,128)(2,1)S(1)}, bf16[32,6912]{1,0:T(8,128)(2,1)}, u32[]{:S(2)}) copy-start(bf16[32,6912]{1,0:T(8,128)(2,1)} %param.13) | copy-start | bytes 1327108
  3.4 107.7 %all-to-all-start.2 = ((bf16[8,2,320]{2,1,0:T(2,128)(2,1)}), bf16[8,2,320]{2,1,0:T(2,128)(2,1)S(1)}, u32[]{:S(2)}, u32[]{:S(2)}) async-start(bf16[8,2,320]{2,1,0:T(2,128)(2,1)} %reshape.31), calls=%async_computation.2 | async-start | bytes 24576 | tf_op jit(solution)/shard_map/all_to_all | solution.py:36
  111.1 385.6 %all-to-all-start = ((bf16[1280,4,1728]{0,2,1:T(8,128)(2,1)}), bf16[1280,4,1728]{0,2,1:T(8,128)(2,1)}, u32[]{:S(2)}, u32[]{:S(2)}) async-start(bf16[1280,4,1728]{0,2,1:T(8,128)(2,1)} %bitcast.13), calls=%async_computation | async-start | bytes 35389440 | tf_op jit(solution)/shard_map/all_to_all | solution.py:27
  496.7 389.3 %all-to-all-start.1 = ((bf16[1280,4,1728]{0,2,1:T(8,128)(2,1)}), bf16[1280,4,1728]{0,2,1:T(8,128)(2,1)}, u32[]{:S(2)}, u32[]{:S(2)}) async-start(bf16[1280,4,1728]{0,2,1:T(8,128)(2,1)} %bitcast.12), calls=%async_computation.1 | async-start | bytes 35389440 | tf_op jit(solution)/shard_map/all_to_all | solution.py:28
  886.0 48.3 %copy-start.1 = (bf16[32,6912]{1,0:T(8,128)(2,1)S(1)}, bf16[32,6912]{1,0:T(8,128)(2,1)}, u32[]{:S(2)}) copy-start(bf16[32,6912]{1,0:T(8,128)(2,1)} %param.10) | copy-start | bytes 1327108
